TPU v7x, 32 devices: a whole 2x2x4 slice. The times are simulated.
32 devices in a mesh: rep: 4 (over x, y), dp: 8 (over z, core).
Axes of the slice: x: 2, y: 2, z: 4, core: 2. Of those that a mesh axis runs over, the one named last changes fastest.
Arguments:
- g_w_gate: bfloat16 [32, 2, 512, 8192], P(('rep', 'dp')), parts along dimension 0
- g_w_up: bfloat16 [32, 2, 512, 8192], P(('rep', 'dp')), parts along dimension 0
- g_w_down: bfloat16 [32, 2, 8192, 512], P(('rep', 'dp')), parts along dimension 0
- w_gate: bfloat16 [2, 512, 8192], replicated
- w_up: bfloat16 [2, 512, 8192], replicated
- w_down: bfloat16 [2, 8192, 512], replicated
- m_w_gate: float32 [2, 512, 8192], P(None, 'dp')
- m_w_up: float32 [2, 512, 8192], P(None, 'dp')
- m_w_down: float32 [2, 8192, 512], P(None, 'dp')
- v_w_gate: float32 [2, 512, 8192], P(None, 'dp')
- v_w_up: float32 [2, 512, 8192], P(None, 'dp')
- v_w_down: float32 [2, 8192, 512], P(None, 'dp')
Outputs:
- output 1: bfloat16 [8, 512, 8192], P('rep'), parts along dimension 0
- output 2: bfloat16 [8, 512, 8192], P('rep'), parts along dimension 0
- output 3: bfloat16 [8, 8192, 512], P('rep'), parts along dimension 0
- output 4: float32 [8, 512, 8192], P('rep', 'dp'), parts along dimension 0
- output 5: float32 [8, 512, 8192], P('rep', 'dp'), parts along dimension 0
- output 6: float32 [8, 8192, 512], P('rep', 'dp'), parts along dimension 0
- output 7: float32 [8, 512, 8192], P('rep', 'dp'), parts along dimension 0
- output 8: float32 [8, 512, 8192], P('rep', 'dp'), parts along dimension 0
- output 9: float32 [8, 8192, 512], P('rep', 'dp'), parts along dimension 0
There are 4 independent parts. A program takes and returns all parts, laid end to end along the dimension named above; an argument that names none is the same for every part.
All inputs are finite; a program needn't handle non-finite values.
Results may differ from a plain program's by a relative error of at most 0.022.
Values are sent between devices in bfloat16 or wider.
A program may use at most 2 GiB of HBM per device.

v0:
```python
import jax
import jax.numpy as jnp
from jax import lax
from jax.sharding import PartitionSpec as P


def adamw(w, m, v, g):
    m = 0.9 * m + 0.1 * g
    v = 0.95 * v + 0.05 * g * g
    step = m * lax.rsqrt(v + 1e-8) + 0.1 * w
    return (w - 0.02 * step).astype(jnp.bfloat16), m, v


def solution(mesh):
    def step(*arrays):
        terms, weights, m, v = (arrays[i : i + 3] for i in (0, 3, 6, 9))
        gradients = [lax.psum_scatter(t[0], "dp", scatter_dimension=1, tiled=True).astype(jnp.float32) for t in terms]
        me = lax.axis_index("dp")
        own = [lax.dynamic_slice_in_dim(w, me * one.shape[1], one.shape[1], 1).astype(jnp.float32) for w, one in zip(weights, m, strict=True)]
        new = [adamw(w, m, v, g) for w, m, v, g in zip(own, m, v, gradients, strict=True)]
        whole = [lax.all_gather(one[0], "dp", axis=1, tiled=True) for one in new]
        return (*whole, *(one[1] for one in new), *(one[2] for one in new))

    all_of, cut = P(None, None, None), P(None, "dp", None)
    return jax.shard_map(
        step,
        mesh=mesh,
        in_specs=(P(("rep", "dp"), None, None, None),) * 3 + (all_of,) * 3 + (cut,) * 6,
        out_specs=(P("rep", None, None),) * 3 + (P("rep", "dp", None),) * 6,
        check_vma=False,
    )
```

profile of v0, /device:TPU:0, one launch (start us, length us, event | category | flops | bytes accessed | tf_op | source)
XLA Modules:
  0.0 1015.7 jit_solution(16835236515173734334)
XLA Ops:
  7.2 0.0 reduce-scatter.8.cloned.1.call-start
  7.2 0.7 reduce-scatter.8.cloned.1.call-update
  7.9 0.0 reduce-scatter.6.cloned.1.call-start
  8.0 0.7 reduce-scatter.6.cloned.1.call-update
  8.7 0.0 reduce-scatter.4.cloned.1.call-start
  8.7 0.7 reduce-scatter.4.cloned.1.call-update
  9.4 0.0 all-gather.8.cloned.1.call-start
  9.4 171.7 %reduce-scatter.8.cloned.1.call-done = bf16[2,1024,512]{2,1,0:T(8,128)(2,1)} async-done(((bf16[2,8192,512]{2,1,0:T(8,128)(2,1)}), bf16[2,1024,512]{2,1,0:T(8,128)(2,1)}) %reduce-scatter.8.cloned.1.call-update) | async-done | bytes 2097168 | tf_op jit(solution)/shard_map/reduce_scatter | solution.py:17
  181.1 8.3 fusion.10
  189.4 0.0 all-gather.8.cloned.1.call-update
  189.4 0.0 all-gather.6.cloned.1.call-start
  189.5 160.8 %reduce-scatter.6.cloned.1.call-done = bf16[2,64,8192]{2,1,0:T(8,128)(2,1)} async-done(((bf16[2,512,8192]{2,1,0:T(8,128)(2,1)}), bf16[2,64,8192]{2,1,0:T(8,128)(2,1)}) %reduce-scatter.6.cloned.1.call-update) | async-done | bytes 2097168 | tf_op jit(solution)/shard_map/reduce_scatter | solution.py:17
  350.3 8.4 fusion.6
  358.7 0.0 all-gather.6.cloned.1.call-update
  358.7 0.0 all-gather.4.cloned.1.call-start
  358.7 160.7 %reduce-scatter.4.cloned.1.call-done = bf16[2,64,8192]{2,1,0:T(8,128)(2,1)} async-done(((bf16[2,512,8192]{2,1,0:T(8,128)(2,1)}), bf16[2,64,8192]{2,1,0:T(8,128)(2,1)}) %reduce-scatter.4.cloned.1.call-update) | async-done | bytes 2097168 | tf_op jit(solution)/shard_map/reduce_scatter | solution.py:17
  519.4 8.4 fusion.2
  527.8 0.0 all-gather.4.cloned.1.call-update
  527.8 143.4 %all-gather.8.cloned.1.call-done = bf16[2,8192,512]{2,1,0:T(8,128)(2,1)} async-done(((bf16[2,1024,512]{2,1,0:T(8,128)(2,1)}), bf16[2,8192,512]{2,1,0:T(8,128)(2,1)}) %all-gather.8.cloned.1.call-update) | async-done | bytes 16777232 | tf_op jit(solution)/shard_map/all_gather | solution.py:21
  671.2 151.8 %all-gather.6.cloned.1.call-done = bf16[2,512,8192]{2,1,0:T(8,128)(2,1)} async-done(((bf16[2,64,8192]{2,1,0:T(8,128)(2,1)}), bf16[2,512,8192]{2,1,0:T(8,128)(2,1)}) %all-gather.6.cloned.1.call-update) | async-done | bytes 16777232 | tf_op jit(solution)/shard_map/all_gather | solution.py:21
  823.0 151.8 %all-gather.4.cloned.1.call-done = bf16[2,512,8192]{2,1,0:T(8,128)(2,1)} async-done(((bf16[2,64,8192]{2,1,0:T(8,128)(2,1)}), bf16[2,512,8192]{2,1,0:T(8,128)(2,1)}) %all-gather.4.cloned.1.call-update) | async-done | bytes 16777232 | tf_op jit(solution)/shard_map/all_gather | solution.py:21
  974.8 0.0 copy-start
  974.8 0.0 slice-start
  974.8 0.0 slice-start.1
  974.8 16.7 %copy.24 = bf16[2,512,8192]{2,1,0:T(8,128)(2,1)} copy(bf16[2,512,8192]{2,1,0:T(8,128)(2,1)} %all-gather.4.cloned.1.call-done) | data formatting | bytes 33554432
  991.5 0.0 copy-done
  991.5 0.0 slice-start.2
  991.5 0.0 slice-start.3
  991.5 8.5 copy.25
  1000.0 0.0 slice-done
  1000.0 0.0 slice-done.1
  1000.0 1.5 slice-done.2
  1001.5 1.2 slice-done.3
  1002.7 6.2 copy.26
  (1 shorter events, 0.0 us)
Async XLA Ops:
  7.2 173.9 %reduce-scatter.8.cloned.1.call-start = ((), (), s32[]{:S(2)}) async-start(), calls=%async_computation.7 | async-start | bytes 18874368 | tf_op jit(solution)/shard_map/reduce_scatter | solution.py:17
  7.9 342.3 %reduce-scatter.6.cloned.1.call-start = ((), (), s32[]{:S(2)}) async-start(), calls=%async_computation.5 | async-start | bytes 18874368 | tf_op jit(solution)/shard_map/reduce_scatter | solution.py:17
  8.7 510.7 %reduce-scatter.4.cloned.1.call-start = ((), (), s32[]{:S(2)}) async-start(), calls=%async_computation.3 | async-start | bytes 18874368 | tf_op jit(solution)/shard_map/reduce_scatter | solution.py:17
  9.4 661.8 %all-gather.8.cloned.1.call-start = ((), (), s32[]{:S(2)}) async-start(), calls=%async_computation.8 | async-start | bytes 18874368 | tf_op jit(solution)/shard_map/all_gather | solution.py:21
  189.4 633.6 %all-gather.6.cloned.1.call-start = ((), (), s32[]{:S(2)}) async-start(), calls=%async_computation.6 | async-start | bytes 18874368 | tf_op jit(solution)/shard_map/all_gather | solution.py:21
  358.7 616.1 %all-gather.4.cloned.1.call-start = ((), (), s32[]{:S(2)}) async-start(), calls=%async_computation.4 | async-start | bytes 18874368 | tf_op jit(solution)/shard_map/all_gather | solution.py:21
  974.8 16.7 %copy-start = (bf16[2,512,8192]{2,1,0:T(8,128)(2,1)S(1)}, bf16[2,512,8192]{2,1,0:T(8,128)(2,1)}, u32[]{:S(2)}) copy-start(bf16[2,512,8192]{2,1,0:T(8,128)(2,1)} %all-gather.6.cloned.1.call-done) | copy-start | bytes 50331652
  974.8 25.2 %slice-start = ((s8[16777216]{0:T(1024)(128)(4,1)}), s8[4194304]{0:T(1024)(128)(4,1)S(1)}, s32[]{:S(2)}) async-start(s8[16777216]{0:T(1024)(128)(4,1)} %bitcast.6), calls=%async_computation.9 | async-start | bytes 8388608
  974.8 25.2 %slice-start.1 = ((s8[16777216]{0:T(1024)(128)(4,1)}), s8[4194304]{0:T(1024)(128)(4,1)S(1)}, s32[]{:S(2)}) async-start(s8[16777216]{0:T(1024)(128)(4,1)} %bitcast.6), calls=%async_computation.10 | async-start | bytes 8388608
  991.5 10.0 slice-start.2
  991.5 11.2 %slice-start.3 = ((s8[16777216]{0:T(1024)(128)(4,1)}), s8[4194304]{0:T(1024)(128)(4,1)S(1)}, s32[]{:S(2)}) async-start(s8[16777216]{0:T(1024)(128)(4,1)} %bitcast.6), calls=%async_computation.12 | async-start | bytes 8388608
Sparse Core Ops, SparseCore 0:
  10.3 170.7 reduce-scatter.7
  183.5 166.7 reduce-scatter.5
  352.6 166.7 reduce-scatter.3
  521.4 149.7 all-gather.7
  673.2 149.7 all-gather.5
  825.1 149.7 all-gather.3
where the time goes:
time: 1020 us
  waiting for transfers between devices  942 us (92%)
  local copies, waits for them, and re-layouts  34.1 us (3%)
  other arithmetic  25.1 us (2%)
  between operations  14.1 us (1%)
    reduce_scatter x3, waiting for transfers between devices, step(): lax.psum_scatter(t[0], 'dp', scatter_dimension=1, tiled=True)  493 us
    all_gather x3, waiting for transfers between devices, step(): whole = [lax.all_gather(one[0], 'dp', axis=1, tiled=True) for one in new]  447 us
    unnamed x13, local copies, waits for them, and re-layouts  34.1 us
    convert_element_type x3, other arithmetic, adamw(): return ((w - 0.02 * step).astype(jnp.bfloat16), m, v)  25.1 us
  transfers between devices with their start and end apart: 6, of which 6 were waited for; matrix products, arithmetic and copies ran while one was open for 2% of the time, Pallas kernels for 0%

commit v1 on v0

v1 whole, which is shorter than its diff:
```python
import functools

import jax
import jax.numpy as jnp
from jax import lax
from jax.experimental import pallas as pl
from jax.experimental.pallas import tpu as pltpu
from jax.sharding import PartitionSpec as P

MESH = pl.DeviceIdType.MESH
CHIPS = 4
LAG = 2
AHEAD = 3
OWN, PAR, ARR, SND, MOM, NEW, GAT = 3, 4, 4, 3, 3, 3, 4
PIECES = 32
SHAPES = ((16, 2048), (16, 2048), (64, 512))


def adamw(w, m, v, g):
    m = 0.9 * m + 0.1 * g
    v = 0.95 * v + 0.05 * g * g
    step = m * lax.rsqrt(v + 1e-8) + 0.1 * w
    return (w - 0.02 * step).astype(jnp.bfloat16), m, v


def piece(ref, w, block, q):
    layer, at = lax.div(q, 16), lax.rem(q, 16)
    if w < 2:
        row = pl.multiple_of(block * 64 + lax.div(at, 4) * 16, 16)
        return ref.at[layer, pl.ds(row, 16), pl.ds(pl.multiple_of(lax.rem(at, 4) * 2048, 2048), 2048)]
    return ref.at[layer, pl.ds(pl.multiple_of(block * 1024 + at * 64, 64), 64), :]


def chunks(w):
    rows, columns = SHAPES[w]
    for r in range(0, rows, 16):
        for c in range(0, columns, 512):
            yield pl.ds(r, 16), pl.ds(c, 512)


def owned_lag(z):
    return LAG * max(z, CHIPS - 1 - z)


def gather_lag(owner, z):
    return owned_lag(owner) + LAG * abs(owner - z)


def kernel(*refs):
    terms, weights, m_in, v_in = (refs[i : i + 3] for i in (0, 3, 6, 9))
    whole, m_out, v_out = (refs[i : i + 3] for i in (12, 15, 18))
    (own_a, own_b, par_a, par_b, arr_a, arr_b, snd_a, snd_b, m_a, m_b, v_a, v_b, w_a, w_b, mo_a, mo_b, vo_a, vo_b, new_a, new_b) = refs[21:41]
    (own_sem, par_recv, par_send, arr_sem, snd_sem, m_sem, v_sem, w_sem, mo_sem, vo_sem, new_sem, gat_recv, gat_send, pal_send, pal_recv) = refs[41:]

    me = lax.axis_index("dp")
    core = lax.rem(me, 2)
    chip = lax.div(me, 2)
    partner = me + 1 - 2 * core

    def slot(a, b, w, n, *lead):
        return a.at[(*lead, w, n)] if w < 2 else b.at[(*lead, n)]

    def remote(src, dst, send, recv, to):
        return pltpu.make_async_remote_copy(src_ref=src, dst_ref=dst, send_sem=send, recv_sem=recv, device_id={"dp": to}, device_id_type=MESH)

    def body(z):
        left, right = z > 0, z < CHIPS - 1
        others = sorted((o for o in range(CHIPS) if o != z), key=lambda o: -abs(o - z))
        neighbours = [partner] + ([me - 2] if left else []) + ([me + 2] if right else [])

        def upstream(o):
            return left if o > z else right

        for o in others:
            if not upstream(o):
                arr_a[o] = jnp.zeros_like(arr_a[o])
                arr_b[o] = jnp.zeros_like(arr_b[o])
        for o, there in ((z, left), (CHIPS, right)):
            if not there:
                arr_a[o] = jnp.zeros_like(arr_a[o])
                arr_b[o] = jnp.zeros_like(arr_b[o])

        barrier = pltpu.get_barrier_semaphore()
        for other in neighbours:
            pl.semaphore_signal(barrier, inc=1, device_id={"dp": other}, device_id_type=MESH)
        pl.semaphore_wait(barrier, len(neighbours))

        def lag(o):
            return owned_lag(z) if o == z else LAG * (z if o > z else CHIPS - 1 - z)

        def own_copy(w, q, o):
            n = lax.rem(q, OWN)
            return pltpu.make_async_copy(piece(terms[w], w, 2 * o + core, q), slot(own_a, own_b, w, n, o), own_sem.at[o, w, n])

        def par_copy(w, q, o):
            n = lax.rem(q, PAR)
            return remote(piece(terms[w], w, 2 * o + 1 - core, q), slot(par_a, par_b, w, n, o), par_send.at[o, w, n], par_recv.at[o, w, n], partner)

        def sum_copy(w, q, o):
            n, k = lax.rem(q, SND), lax.rem(q, ARR)
            way = 1 if o > z else -1
            there = CHIPS if way < 0 and o == z - 1 else o
            return remote(slot(snd_a, snd_b, w, n, o), slot(arr_a, arr_b, w, k, there), snd_sem.at[o, w, n], arr_sem.at[there, w, k], me + 2 * way)

        def arr_wait(w, q, o):
            k = lax.rem(q, ARR)
            there = slot(arr_a, arr_b, w, k, o)
            remote(there, there, snd_sem.at[0, w, 0], arr_sem.at[o, w, k], me).wait_recv()

        def state_copies(w, q):
            n = lax.rem(q, MOM)
            return (
                pltpu.make_async_copy(piece(m_in[w], w, 0, q), slot(m_a, m_b, w, n), m_sem.at[w, n]),
                pltpu.make_async_copy(piece(v_in[w], w, 0, q), slot(v_a, v_b, w, n), v_sem.at[w, n]),
                pltpu.make_async_copy(piece(weights[w], w, me, q), slot(w_a, w_b, w, n), w_sem.at[w, n]),
            )

        def result_copies(w, q):
            n, k = lax.rem(q, NEW), lax.rem(q, GAT)
            new, there = slot(new_a, new_b, w, n), piece(whole[w], w, me, q)
            local = [
                pltpu.make_async_copy(slot(mo_a, mo_b, w, n), piece(m_out[w], w, 0, q), mo_sem.at[w, n]),
                pltpu.make_async_copy(slot(vo_a, vo_b, w, n), piece(v_out[w], w, 0, q), vo_sem.at[w, n]),
                pltpu.make_async_copy(new, there, new_sem.at[0, w, n]),
            ]
            far = [remote(new, there, new_sem.at[1, w, n], gat_recv.at[z, w, k], me + 2)] if right else []
            far += [remote(new, there, new_sem.at[2, w, n], gat_recv.at[z, w, k], me - 2)] if left else []
            far += [remote(new, there, new_sem.at[3, w, n], pal_recv.at[w], partner)]
            return local, far

        def pass_copies(w, q, o):
            k = lax.rem(q, GAT)
            there = piece(whole[w], w, 2 * o + core, q)
            way = -1 if o > z else 1
            on = left if o > z else right
            far = [remote(there, there, gat_send.at[o, w, k], gat_recv.at[o, w, k], me + 2 * way)] if on else []
            return far + [remote(there, there, pal_send.at[o, w, k], pal_recv.at[w], partner)]

        def pass_wait(w, q, o):
            k = lax.rem(q, GAT)
            there = piece(whole[w], w, 2 * o + core, q)
            remote(there, there, gat_send.at[o, w, k], gat_recv.at[o, w, k], me).wait_recv()

        def at(i, k, lag):
            w = (k - lag) % 3
            return w, i + (k - lag - w) // 3

        def valid(q):
            return (q >= 0) & (q < PIECES)

        def fetch(i, k):
            for o in (*others, z):
                w, q = at(i, k, lag(o) - AHEAD)

                @pl.when(valid(q))
                def _(w=w, q=q, o=o):
                    @pl.when(q >= PAR)
                    def _():
                        par_copy(w, q - PAR, o).wait_send()

                    par_copy(w, q, o).start()
                    own_copy(w, q, o).start()
                    if o == z:
                        for copy in state_copies(w, q):
                            copy.start()

        def forward(i, k, o):
            w, q = at(i, k, lag(o))

            @pl.when(valid(q))
            def _():
                own_copy(w, q, o).wait()
                par_copy(w, q, o).wait_recv()
                if upstream(o):
                    arr_wait(w, q, o)

                @pl.when(q >= SND)
                def _():
                    sum_copy(w, q - SND, o).wait_send()

                own, par = slot(own_a, own_b, w, lax.rem(q, OWN), o), slot(par_a, par_b, w, lax.rem(q, PAR), o)
                arr, snd = slot(arr_a, arr_b, w, lax.rem(q, ARR), o), slot(snd_a, snd_b, w, lax.rem(q, SND), o)
                for r, c in chunks(w):
                    total = own[r, c].astype(jnp.float32) + par[r, c].astype(jnp.float32) + arr[r, c].astype(jnp.float32)
                    snd[r, c] = total.astype(jnp.bfloat16)
                sum_copy(w, q, o).start()

        def finish(i, k):
            w, q = at(i, k, lag(z))

            @pl.when(valid(q))
            def _():
                own_copy(w, q, z).wait()
                par_copy(w, q, z).wait_recv()
                for copy in state_copies(w, q):
                    copy.wait()
                if left:
                    arr_wait(w, q, z)
                if right:
                    arr_wait(w, q, CHIPS)

                @pl.when(q >= NEW)
                def _():
                    drain_result(w, q - NEW)

                own, par = slot(own_a, own_b, w, lax.rem(q, OWN), z), slot(par_a, par_b, w, lax.rem(q, PAR), z)
                one, two = slot(arr_a, arr_b, w, lax.rem(q, ARR), z), slot(arr_a, arr_b, w, lax.rem(q, ARR), CHIPS)
                n, k = lax.rem(q, MOM), lax.rem(q, NEW)
                m, v, old = slot(m_a, m_b, w, n), slot(v_a, v_b, w, n), slot(w_a, w_b, w, n)
                mo, vo, new = slot(mo_a, mo_b, w, k), slot(vo_a, vo_b, w, k), slot(new_a, new_b, w, k)
                for r, c in chunks(w):
                    total = own[r, c].astype(jnp.float32) + par[r, c].astype(jnp.float32)
                    total = total + one[r, c].astype(jnp.float32) + two[r, c].astype(jnp.float32)
                    g = total.astype(jnp.bfloat16).astype(jnp.float32)
                    new[r, c], mo[r, c], vo[r, c] = adamw(old[r, c].astype(jnp.float32), m[r, c], v[r, c], g)
                local, far = result_copies(w, q)
                for copy in (*far, *local):
                    copy.start()

        def drain_result(w, q):
            local, far = result_copies(w, q)
            for copy in local:
                copy.wait()
            for copy in far:
                copy.wait_send()

        def pass_on(i, k, o):
            w, q = at(i, k, gather_lag(o, z))

            @pl.when(valid(q))
            def _():
                pass_wait(w, q, o)

                @pl.when(q >= GAT)
                def _():
                    for copy in pass_copies(w, q - GAT, o):
                        copy.wait_send()

                for copy in pass_copies(w, q, o):
                    copy.start()

        last = 3 * PIECES + max(gather_lag(o, z) for o in range(CHIPS))

        @pl.loop(-(AHEAD // 3), -(-last // 3))
        def _(i):
            for k in range(3):
                fetch(i, k)
                for o in others:
                    forward(i, k, o)
                finish(i, k)
                for o in others:
                    pass_on(i, k, o)

        def tail(ring, wait):
            @pl.loop(PIECES - ring, PIECES)
            def _(q):
                for w in range(3):
                    wait(w, q)

        def tail_par(w, q):
            for o in range(CHIPS):
                par_copy(w, q, o).wait_send()

        def tail_sum(w, q):
            for o in others:
                sum_copy(w, q, o).wait_send()

        def tail_pass(w, q):
            for o in others:
                for copy in pass_copies(w, q, o):
                    copy.wait_send()

        tail(PAR, tail_par)
        tail(SND, tail_sum)
        tail(NEW, drain_result)
        tail(GAT, tail_pass)
        for w in range(3):
            half = whole[w].at[0]
            pltpu.make_async_copy(half, half, pal_recv.at[w]).wait()

    for z in range(CHIPS):

        @pl.when(chip == z)
        def _(z=z):
            body(z)


def communicate(terms, weights, m, v):
    def ring(dtype, *lead):
        return [pltpu.VMEM((*lead[:-1], 2, lead[-1], *SHAPES[0]), dtype), pltpu.VMEM((*lead, *SHAPES[2]), dtype)]

    dma = pltpu.SemaphoreType.DMA
    bf16, f32 = jnp.bfloat16, jnp.float32
    return pl.pallas_call(
        kernel,
        out_shape=[jax.ShapeDtypeStruct(a.shape, a.dtype) for a in (*weights, *m, *v)],
        in_specs=[pl.BlockSpec(memory_space=pl.ANY)] * 12,
        out_specs=[pl.BlockSpec(memory_space=pl.ANY)] * 9,
        scratch_shapes=[
            *ring(bf16, CHIPS, OWN),
            *ring(bf16, CHIPS, PAR),
            *ring(bf16, CHIPS + 1, ARR),
            *ring(bf16, CHIPS, SND),
            *ring(f32, MOM),
            *ring(f32, MOM),
            *ring(bf16, MOM),
            *ring(f32, NEW),
            *ring(f32, NEW),
            *ring(bf16, NEW),
            dma((CHIPS, 3, OWN)),
            dma((CHIPS, 3, PAR)),
            dma((CHIPS, 3, PAR)),
            dma((CHIPS + 1, 3, ARR)),
            dma((CHIPS, 3, SND)),
            dma((3, MOM)),
            dma((3, MOM)),
            dma((3, MOM)),
            dma((3, NEW)),
            dma((3, NEW)),
            dma((4, 3, NEW)),
            dma((CHIPS, 3, GAT)),
            dma((CHIPS, 3, GAT)),
            dma((CHIPS, 3, GAT)),
            dma((3,)),
        ],
        compiler_params=pltpu.CompilerParams(collective_id=0, has_side_effects=True),
        name="sum_step_gather",
    )(*terms, *weights, *m, *v)


def hand_out(arrays):
    steps = 16

    def spec(a):
        _, rows, columns = a.shape
        return pl.BlockSpec((1, rows * 2 // steps, columns), lambda i: (lax.div(i, steps // 2), lax.rem(i, steps // 2), 0))

    def copy(*refs):
        for i, o in zip(refs[:9], refs[9:], strict=True):
            o[...] = i[...]

    return pl.pallas_call(
        copy,
        grid=(steps,),
        out_shape=[jax.ShapeDtypeStruct(a.shape, a.dtype) for a in arrays],
        in_specs=[spec(a) for a in arrays],
        out_specs=[spec(a) for a in arrays],
        name="hand_out",
    )(*arrays)


def solution(mesh):
    def step(*arrays):
        terms, weights, m, v = (arrays[i : i + 3] for i in (0, 3, 6, 9))
        terms = [t.reshape(t.shape[1:]) for t in terms]
        return tuple(hand_out(communicate(terms, weights, m, v)))

    all_of, cut = P(None, None, None), P(None, "dp", None)
    return jax.shard_map(
        step,
        mesh=mesh,
        in_specs=(P(("rep", "dp"), None, None, None),) * 3 + (all_of,) * 3 + (cut,) * 6,
        out_specs=(P("rep", None, None),) * 3 + (P("rep", "dp", None),) * 6,
        check_vma=False,
    )
```

time: 1020 us -> 617 us (0.60)
  waiting for transfers between devices: 942 us -> 0 us
  Pallas kernels: 0 us -> 617 us
  local copies, waits for them, and re-layouts: 34.1 us -> 0 us
  other arithmetic: 25.1 us -> 0 us
  between operations: 14.1 us -> 0.65 us
    pallas_call x0 -> x2, Pallas kernels: none -> 617 us  [the longest x1 568 us: communicate(): pl.pallas_call(kernel, out_shape=[jax.ShapeDtypeStruct(a.shape, a.dtype)...]
    reduce_scatter x3 -> x0, waiting for transfers between devices: 493 us -> none  [step(): lax.psum_scatter(t[0], 'dp', scatter_dimension=1, tiled=True)]
    all_gather x3 -> x0, waiting for transfers between devices: 447 us -> none  [step(): whole = [lax.all_gather(one[0], 'dp', axis=1, tiled=True) for one in new]]
    unnamed x13 -> x0, local copies, waits for them, and re-layouts: 34.1 us -> none
    convert_element_type x3 -> x0, other arithmetic: 25.1 us -> none  [adamw(): return ((w - 0.02 * step).astype(jnp.bfloat16), m, v)]
  transfers between devices with their start and end apart: 6 -> 0, of which waited for: 6 -> 0; matrix products, arithmetic and copies ran while one was open for 2% -> 0% of each run, Pallas kernels for 0% -> 0%
where the time goes in v1:
time: 617 us
  Pallas kernels  617 us (100%)
    pallas_call x1, Pallas kernels, communicate(): pl.pallas_call(kernel, out_shape=[jax.ShapeDtypeStruct(a.shape, a.dtype)...  568 us
    pallas_call x1, Pallas kernels, hand_out(): pl.pallas_call(copy, grid=(steps,), out_shape=[jax.ShapeDtypeStruct(a.sha...  48.3 us

profile of v1, /device:TPU:0, one launch (start us, length us, event | category | flops | bytes accessed | tf_op | source)
XLA Modules:
  0.0 617.2 jit_solution(7536563704103096577)
XLA Ops:
  0.6 568.3 %sum_step_gather.1 = (bf16[2,512,8192]{2,1,0:T(8,128)(2,1)}, bf16[2,512,8192]{2,1,0:T(8,128)(2,1)}, bf16[2,8192,512]{2,1,0:T(8,128)(2,1)}, f32[2,64,8192]{2,1,0:...) custom-call(bf16[2,512,8192]{2,1,0:T(8,128)(2,1)} %bitcast.3, ...), custom_call_target="tpu_custom_call" | custom-call | tf_op jit(solution)/shard_map/sum_step_gather/pallas_call | solution.py:294
  569.0 48.3 %hand_out.1 = (bf16[2,512,8192]{2,1,0:T(8,128)(2,1)}, bf16[2,512,8192]{2,1,0:T(8,128)(2,1)}, bf16[2,8192,512]{2,1,0:T(8,128)(2,1)}, f32[2,64,8192]{2,1,0:T(8,128...) custom-call(bf16[2,512,8192]{2,1,0:T(8,128)(2,1)} %get-tuple-element, ...), custom_call_target="tpu_custom_call" | custom-call | tf_op jit(solution)/shard_map/hand_out/pallas_call | solution.py:342

commit v2 on v1

--- a/solution.py
+++ b/solution.py
@@ -9,9 +9,10 @@
 
 MESH = pl.DeviceIdType.MESH
 CHIPS = 4
-LAG = 2
+LIMIT = 14 << 20
+LAG = 1
 AHEAD = 3
-OWN, PAR, ARR, SND, MOM, NEW, GAT = 3, 4, 4, 3, 3, 3, 4
+OWN, PAR, ARR, SND, MOM, NEW, GAT = 2, 3, 3, 2, 2, 2, 4
 PIECES = 32
 SHAPES = ((16, 2048), (16, 2048), (64, 512))
 
@@ -49,8 +50,8 @@
 def kernel(*refs):
     terms, weights, m_in, v_in = (refs[i : i + 3] for i in (0, 3, 6, 9))
     whole, m_out, v_out = (refs[i : i + 3] for i in (12, 15, 18))
-    (own_a, own_b, par_a, par_b, arr_a, arr_b, snd_a, snd_b, m_a, m_b, v_a, v_b, w_a, w_b, mo_a, mo_b, vo_a, vo_b, new_a, new_b) = refs[21:41]
-    (own_sem, par_recv, par_send, arr_sem, snd_sem, m_sem, v_sem, w_sem, mo_sem, vo_sem, new_sem, gat_recv, gat_send, pal_send, pal_recv) = refs[41:]
+    (own_a, own_b, par_a, par_b, arr_a, arr_b, snd_a, snd_b, m_a, m_b, v_a, v_b, w_a, w_b, mo_a, mo_b, vo_a, vo_b) = refs[21:39]
+    (own_sem, par_recv, par_send, arr_sem, snd_sem, m_sem, v_sem, w_sem, mo_sem, vo_sem, new_sem, gat_recv, gat_send, pal_send, pal_recv) = refs[39:]
 
     me = lax.axis_index("dp")
     core = lax.rem(me, 2)
@@ -117,15 +118,14 @@
 
         def result_copies(w, q):
             n, k = lax.rem(q, NEW), lax.rem(q, GAT)
-            new, there = slot(new_a, new_b, w, n), piece(whole[w], w, me, q)
+            there = piece(whole[w], w, me, q)
             local = [
                 pltpu.make_async_copy(slot(mo_a, mo_b, w, n), piece(m_out[w], w, 0, q), mo_sem.at[w, n]),
                 pltpu.make_async_copy(slot(vo_a, vo_b, w, n), piece(v_out[w], w, 0, q), vo_sem.at[w, n]),
-                pltpu.make_async_copy(new, there, new_sem.at[0, w, n]),
             ]
-            far = [remote(new, there, new_sem.at[1, w, n], gat_recv.at[z, w, k], me + 2)] if right else []
-            far += [remote(new, there, new_sem.at[2, w, n], gat_recv.at[z, w, k], me - 2)] if left else []
-            far += [remote(new, there, new_sem.at[3, w, n], pal_recv.at[w], partner)]
+            far = [remote(there, there, new_sem.at[0, w, n], gat_recv.at[z, w, k], me + 2)] if right else []
+            far += [remote(there, there, new_sem.at[1, w, n], gat_recv.at[z, w, k], me - 2)] if left else []
+            far += [remote(there, there, new_sem.at[2, w, n], pal_recv.at[w], partner)]
             return local, far
 
         def pass_copies(w, q, o):
@@ -207,7 +207,7 @@
                 one, two = slot(arr_a, arr_b, w, lax.rem(q, ARR), z), slot(arr_a, arr_b, w, lax.rem(q, ARR), CHIPS)
                 n, k = lax.rem(q, MOM), lax.rem(q, NEW)
                 m, v, old = slot(m_a, m_b, w, n), slot(v_a, v_b, w, n), slot(w_a, w_b, w, n)
-                mo, vo, new = slot(mo_a, mo_b, w, k), slot(vo_a, vo_b, w, k), slot(new_a, new_b, w, k)
+                mo, vo, new = slot(mo_a, mo_b, w, k), slot(vo_a, vo_b, w, k), piece(whole[w], w, me, q)
                 for r, c in chunks(w):
                     total = own[r, c].astype(jnp.float32) + par[r, c].astype(jnp.float32)
                     total = total + one[r, c].astype(jnp.float32) + two[r, c].astype(jnp.float32)
@@ -293,9 +293,9 @@
     bf16, f32 = jnp.bfloat16, jnp.float32
     return pl.pallas_call(
         kernel,
-        out_shape=[jax.ShapeDtypeStruct(a.shape, a.dtype) for a in (*weights, *m, *v)],
+        out_shape=[pltpu.VMEM(a.shape, a.dtype) for a in weights] + [jax.ShapeDtypeStruct(a.shape, a.dtype) for a in (*m, *v)],
         in_specs=[pl.BlockSpec(memory_space=pl.ANY)] * 12,
-        out_specs=[pl.BlockSpec(memory_space=pl.ANY)] * 9,
+        out_specs=[pl.BlockSpec(memory_space=pltpu.VMEM)] * 3 + [pl.BlockSpec(memory_space=pl.ANY)] * 6,
         scratch_shapes=[
             *ring(bf16, CHIPS, OWN),
             *ring(bf16, CHIPS, PAR),
@@ -306,7 +306,6 @@
             *ring(bf16, MOM),
             *ring(f32, NEW),
             *ring(f32, NEW),
-            *ring(bf16, NEW),
             dma((CHIPS, 3, OWN)),
             dma((CHIPS, 3, PAR)),
             dma((CHIPS, 3, PAR)),
@@ -317,36 +316,64 @@
             dma((3, MOM)),
             dma((3, NEW)),
             dma((3, NEW)),
-            dma((4, 3, NEW)),
+            dma((3, 3, NEW)),
             dma((CHIPS, 3, GAT)),
             dma((CHIPS, 3, GAT)),
             dma((CHIPS, 3, GAT)),
             dma((3,)),
         ],
-        compiler_params=pltpu.CompilerParams(collective_id=0, has_side_effects=True),
+        compiler_params=pltpu.CompilerParams(collective_id=0, has_side_effects=True, vmem_limit_bytes=LIMIT),
         name="sum_step_gather",
     )(*terms, *weights, *m, *v)
 
 
 def hand_out(arrays):
-    steps = 16
-
-    def spec(a):
-        _, rows, columns = a.shape
-        return pl.BlockSpec((1, rows * 2 // steps, columns), lambda i: (lax.div(i, steps // 2), lax.rem(i, steps // 2), 0))
+    slots = (8, 4)
 
     def copy(*refs):
-        for i, o in zip(refs[:9], refs[9:], strict=True):
-            o[...] = i[...]
-
+        held, moments, whole, out = refs[:3], refs[3:9], refs[9:12], refs[12:18]
+        buffers, into, out_of, sent = refs[18:20], refs[20], refs[21], refs[22]
+        down = [pltpu.make_async_copy(held[w].at[l], whole[w].at[l], sent.at[w, l]) for w in range(3) for l in range(2)]
+        jobs, used = [], [0, 0]
+        for l in range(2):
+            for half in range(2):
+                for n in range(6):
+                    kind = n % 3 // 2
+                    rows = pl.ds(half * (32, 512)[kind], (32, 512)[kind])
+                    slot = used[kind] % slots[kind]
+                    jobs.append((
+                        (kind, slot),
+                        pltpu.make_async_copy(moments[n].at[l, rows], buffers[kind].at[slot], into.at[kind, slot]),
+                        pltpu.make_async_copy(buffers[kind].at[slot], out[n].at[l, rows], out_of.at[kind, slot]),
+                    ))
+                    used[kind] += 1
+        ahead = sum(slots)
+        for _, load, _ in jobs[:ahead]:
+            load.start()
+        for weight in down:
+            weight.start()
+        for n, (_, load, store) in enumerate(jobs):
+            load.wait()
+            store.start()
+            if n >= 4 and n - 4 + ahead < len(jobs):
+                jobs[n - 4][2].wait()
+                jobs[n - 4 + ahead][1].start()
+        for n, (_, _, store) in enumerate(jobs):
+            if n + ahead >= len(jobs):
+                store.wait()
+        for weight in down:
+            weight.wait()
+
+    dma = pltpu.SemaphoreType.DMA
     return pl.pallas_call(
         copy,
-        grid=(steps,),
         out_shape=[jax.ShapeDtypeStruct(a.shape, a.dtype) for a in arrays],
-        in_specs=[spec(a) for a in arrays],
-        out_specs=[spec(a) for a in arrays],
+        in_specs=[pl.BlockSpec(memory_space=pl.ANY)] * 9,
+        out_specs=[pl.BlockSpec(memory_space=pl.ANY)] * 9,
+        scratch_shapes=[pltpu.VMEM((8, 32, 8192), jnp.float32), pltpu.VMEM((4, 512, 512), jnp.float32), dma((2, 8)), dma((2, 8)), dma((3, 2))],
+        compiler_params=pltpu.CompilerParams(vmem_limit_bytes=LIMIT),
         name="hand_out",
-    )(*arrays)
+    )(*[pltpu.with_memory_space_constraint(a, pltpu.VMEM if n < 3 else pltpu.HBM) for n, a in enumerate(arrays)])
 
 
 def solution(mesh):

time: 617 us -> 598 us (0.969)
  Pallas kernels: 617 us -> 597 us
    pallas_call x2, Pallas kernels: 617 us -> 597 us  [the longest x1 563 us: communicate(): pl.pallas_call(kernel, out_shape=[pltpu.VMEM(a.shape, a.dtype) for a in w...]
where the time goes in v2:
time: 598 us; the launch traced here: 597 us
  Pallas kernels  597 us (100%)
    pallas_call x1, Pallas kernels, communicate(): pl.pallas_call(kernel, out_shape=[pltpu.VMEM(a.shape, a.dtype) for a in w...  563 us
    pallas_call x1, Pallas kernels, hand_out(): pl.pallas_call(copy, out_shape=[jax.ShapeDtypeStruct(a.shape, a.dtype) fo...  33.6 us

profile of v2, /device:TPU:0, one launch (start us, length us, event | category | flops | bytes accessed | tf_op | source)
XLA Modules:
  0.0 597.4 jit_solution(8726093593116573324)
XLA Ops:
  0.6 563.2 %sum_step_gather.1 = (bf16[2,512,8192]{2,1,0:T(8,128)(2,1)S(1)}, bf16[2,512,8192]{2,1,0:T(8,128)(2,1)S(1)}, bf16[2,8192,512]{2,1,0:T(8,128)(2,1)S(1)}, f32[2,64,...) custom-call(bf16[2,512,8192]{2,1,0:T(8,128)(2,1)} %bitcast.3, ...), custom_call_target="tpu_custom_call" | custom-call | tf_op jit(solution)/shard_map/sum_step_gather/pallas_call | solution.py:294
  563.9 33.6 %hand_out.1 = (bf16[2,512,8192]{2,1,0:T(8,128)(2,1)}, bf16[2,512,8192]{2,1,0:T(8,128)(2,1)}, bf16[2,8192,512]{2,1,0:T(8,128)(2,1)}, f32[2,64,8192]{2,1,0:T(8,128...) custom-call(bf16[2,512,8192]{2,1,0:T(8,128)(2,1)S(1)} %get-tuple-ele, ...), custom_call_target="tpu_custom_call" | custom-call | tf_op jit(solution)/shard_map/hand_out/pallas_call | solution.py:368

commit v3 on v1

v3 whole, which is shorter than its diff:
```python
import functools

import jax
import jax.numpy as jnp
from jax import lax
from jax.experimental import pallas as pl
from jax.experimental.pallas import tpu as pltpu
from jax.sharding import PartitionSpec as P

MESH = pl.DeviceIdType.MESH
CHIPS = 4
LAG = 2
LEAD = 2
AHEAD = 3
OWN, PAR, ARR, SND, MOM, NEW, GAT = 2, 3, 3, 2, 2, 2, 4
WEIGHTS = 3
PIECES = 64
SHAPES = ((16, 1024), (16, 1024), (32, 512))
KEPT = 2
GRANT = 6 << 20


def adamw(w, m, v, g):
    m = 0.9 * m + 0.1 * g
    v = 0.95 * v + 0.05 * g * g
    step = m * lax.rsqrt(v + 1e-8) + 0.1 * w
    return (w - 0.02 * step).astype(jnp.bfloat16), m, v


def piece(ref, w, block, q):
    layer, at = lax.div(q, 32), lax.rem(q, 32)
    if w < 2:
        row = pl.multiple_of(block * 64 + lax.div(at, 8) * 16, 16)
        return ref.at[layer, pl.ds(row, 16), pl.ds(pl.multiple_of(lax.rem(at, 8) * 1024, 1024), 1024)]
    return ref.at[layer, pl.ds(pl.multiple_of(block * 1024 + at * 32, 32), 32), :]


def chunks(w):
    rows, columns = SHAPES[w]
    for r in range(0, rows, 16):
        for c in range(0, columns, 512):
            yield pl.ds(r, 16), pl.ds(c, 512)


def late(owner):
    return 0 if owner in (0, CHIPS - 1) else LEAD


def owned_lag(z):
    return late(z) + LAG * max(z, CHIPS - 1 - z)


def gather_lag(owner, z):
    return owned_lag(owner) + LAG * abs(owner - z)


def kernel(*refs):
    refs = iter(refs)

    def take(n=WEIGHTS):
        return [next(refs) for _ in range(n)]

    terms, weights, m_in, v_in, whole, m_out, v_out = (take() for _ in range(7))
    own_ring, par_ring, arr_ring, snd_ring, m_ring, v_ring, w_ring = (take() for _ in range(7))
    mo_ring, vo_ring = take(KEPT), take(KEPT)
    own_sem, par_recv, par_send, arr_sem, snd_sem, m_sem, v_sem, w_sem, mo_sem, vo_sem, new_sem, gat_recv, gat_send, pal_send, pal_recv = refs

    me = lax.axis_index("dp")
    core = lax.rem(me, 2)
    chip = lax.div(me, 2)
    partner = me + 1 - 2 * core

    def remote(src, dst, send, recv, to):
        return pltpu.make_async_remote_copy(src_ref=src, dst_ref=dst, send_sem=send, recv_sem=recv, device_id={"dp": to}, device_id_type=MESH)

    def body(z):
        left, right = z > 0, z < CHIPS - 1
        others = sorted((o for o in range(CHIPS) if o != z), key=lambda o: -abs(o - z))
        neighbours = [partner] + ([me - 2] if left else []) + ([me + 2] if right else [])

        def upstream(o):
            return left if o > z else right

        barrier = pltpu.get_barrier_semaphore()
        for other in neighbours:
            pl.semaphore_signal(barrier, inc=1, device_id={"dp": other}, device_id_type=MESH)
        for o, there in (*((o, upstream(o)) for o in others), (z, left), (CHIPS, right)):
            if not there:
                for arr in arr_ring:
                    arr[o] = jnp.zeros_like(arr[o])

        pl.semaphore_wait(barrier, len(neighbours))

        def lag(o):
            return owned_lag(z) if o == z else late(o) + LAG * (z if o > z else CHIPS - 1 - z)

        def own_copy(w, q, o):
            n = lax.rem(q, OWN)
            return pltpu.make_async_copy(piece(terms[w], w, 2 * o + core, q), own_ring[w].at[o, n], own_sem.at[o, w, n])

        def par_copy(w, q, o):
            n = lax.rem(q, PAR)
            return remote(piece(terms[w], w, 2 * o + 1 - core, q), par_ring[w].at[o, n], par_send.at[o, w, n], par_recv.at[o, w, n], partner)

        def sum_copy(w, q, o):
            n, k = lax.rem(q, SND), lax.rem(q, ARR)
            way = 1 if o > z else -1
            there = CHIPS if way < 0 and o == z - 1 else o
            return remote(snd_ring[w].at[o, n], arr_ring[w].at[there, k], snd_sem.at[o, w, n], arr_sem.at[there, w, k], me + 2 * way)

        def arr_wait(w, q, o):
            k = lax.rem(q, ARR)
            there = arr_ring[w].at[o, k]
            remote(there, there, snd_sem.at[0, w, 0], arr_sem.at[o, w, k], me).wait_recv()

        def state_copies(w, q):
            n = lax.rem(q, MOM)
            return (
                pltpu.make_async_copy(piece(m_in[w], w, 0, q), m_ring[w].at[n], m_sem.at[w, n]),
                pltpu.make_async_copy(piece(v_in[w], w, 0, q), v_ring[w].at[n], v_sem.at[w, n]),
                pltpu.make_async_copy(piece(weights[w], w, me, q), w_ring[w].at[n], w_sem.at[w, n]),
            )

        def result_copies(w, q):
            n, k = lax.rem(q, NEW), lax.rem(q, GAT)
            new = there = piece(whole[w], w, me, q)
            local = []
            if w != KEPT:
                local.append(pltpu.make_async_copy(mo_ring[w].at[n], piece(m_out[w], w, 0, q), mo_sem.at[w, n]))
                local.append(pltpu.make_async_copy(vo_ring[w].at[n], piece(v_out[w], w, 0, q), vo_sem.at[w, n]))
            far = [remote(new, there, new_sem.at[0, w, n], gat_recv.at[z, w, k], me + 2)] if right else []
            far += [remote(new, there, new_sem.at[1, w, n], gat_recv.at[z, w, k], me - 2)] if left else []
            far += [remote(new, there, new_sem.at[2, w, n], pal_recv.at[w], partner)]
            return local, far

        def pass_copies(w, q, o):
            k = lax.rem(q, GAT)
            there = piece(whole[w], w, 2 * o + core, q)
            way = -1 if o > z else 1
            on = left if o > z else right
            far = [remote(there, there, gat_send.at[o, w, k], gat_recv.at[o, w, k], me + 2 * way)] if on else []
            return far + [remote(there, there, pal_send.at[o, w, k], pal_recv.at[w], partner)]

        def pass_wait(w, q, o):
            k = lax.rem(q, GAT)
            there = piece(whole[w], w, 2 * o + core, q)
            remote(there, there, gat_send.at[o, w, k], gat_recv.at[o, w, k], me).wait_recv()

        def at(i, k, lag):
            w = (k - lag) % WEIGHTS
            return w, i + (k - lag - w) // WEIGHTS

        def valid(q):
            return (q >= 0) & (q < PIECES)

        def fetch(i, k):
            for o in (*others, z):
                w, q = at(i, k, lag(o) - AHEAD)

                @pl.when(valid(q))
                def _(w=w, q=q, o=o):
                    @pl.when(q >= PAR)
                    def _():
                        par_copy(w, q - PAR, o).wait_send()

                    par_copy(w, q, o).start()
                    own_copy(w, q, o).start()
                    if o == z:
                        for copy in state_copies(w, q):
                            copy.start()

        def forward(i, k, o):
            w, q = at(i, k, lag(o))

            @pl.when(valid(q))
            def _():
                own_copy(w, q, o).wait()
                par_copy(w, q, o).wait_recv()
                if upstream(o):
                    arr_wait(w, q, o)

                @pl.when(q >= SND)
                def _():
                    sum_copy(w, q - SND, o).wait_send()

                own, par = own_ring[w].at[o, lax.rem(q, OWN)], par_ring[w].at[o, lax.rem(q, PAR)]
                arr, snd = arr_ring[w].at[o, lax.rem(q, ARR)], snd_ring[w].at[o, lax.rem(q, SND)]
                for r, c in chunks(w):
                    total = own[r, c].astype(jnp.float32) + par[r, c].astype(jnp.float32) + arr[r, c].astype(jnp.float32)
                    snd[r, c] = total.astype(jnp.bfloat16)
                sum_copy(w, q, o).start()

        def finish(i, k):
            w, q = at(i, k, lag(z))

            @pl.when(valid(q))
            def _():
                own_copy(w, q, z).wait()
                par_copy(w, q, z).wait_recv()
                for copy in state_copies(w, q):
                    copy.wait()
                if left:
                    arr_wait(w, q, z)
                if right:
                    arr_wait(w, q, CHIPS)

                @pl.when(q >= NEW)
                def _():
                    drain_result(w, q - NEW)

                own, par = own_ring[w].at[z, lax.rem(q, OWN)], par_ring[w].at[z, lax.rem(q, PAR)]
                one, two = arr_ring[w].at[z, lax.rem(q, ARR)], arr_ring[w].at[CHIPS, lax.rem(q, ARR)]
                n = lax.rem(q, MOM)
                m, v, old = m_ring[w].at[n], v_ring[w].at[n], w_ring[w].at[n]
                new, k = piece(whole[w], w, me, q), lax.rem(q, NEW)
                if w == KEPT:
                    mo, vo = piece(m_out[w], w, 0, q), piece(v_out[w], w, 0, q)
                else:
                    mo, vo = mo_ring[w].at[k], vo_ring[w].at[k]
                for r, c in chunks(w):
                    total = own[r, c].astype(jnp.float32) + par[r, c].astype(jnp.float32)
                    total = total + one[r, c].astype(jnp.float32) + two[r, c].astype(jnp.float32)
                    g = total.astype(jnp.bfloat16).astype(jnp.float32)
                    new[r, c], mo[r, c], vo[r, c] = adamw(old[r, c].astype(jnp.float32), m[r, c], v[r, c], g)
                local, far = result_copies(w, q)
                for copy in (*far, *local):
                    copy.start()

        def drain_result(w, q):
            local, far = result_copies(w, q)
            for copy in local:
                copy.wait()
            for copy in far:
                copy.wait_send()

        def pass_on(i, k, o):
            w, q = at(i, k, gather_lag(o, z))

            @pl.when(valid(q))
            def _():
                pass_wait(w, q, o)

                @pl.when(q >= GAT)
                def _():
                    for copy in pass_copies(w, q - GAT, o):
                        copy.wait_send()

                for copy in pass_copies(w, q, o):
                    copy.start()

        last = WEIGHTS * PIECES + max(gather_lag(o, z) for o in range(CHIPS))

        @pl.loop(-((AHEAD + WEIGHTS - 1) // WEIGHTS), -(-last // WEIGHTS))
        def _(i):
            for k in range(WEIGHTS):
                fetch(i, k)
                for o in others:
                    forward(i, k, o)
                finish(i, k)
                for o in others:
                    pass_on(i, k, o)

        def tail(ring, wait):
            @pl.loop(PIECES - ring, PIECES)
            def _(q):
                for w in range(WEIGHTS):
                    wait(w, q)

        def tail_par(w, q):
            for o in range(CHIPS):
                par_copy(w, q, o).wait_send()

        def tail_sum(w, q):
            for o in others:
                sum_copy(w, q, o).wait_send()

        def tail_pass(w, q):
            for o in others:
                for copy in pass_copies(w, q, o):
                    copy.wait_send()

        tail(PAR, tail_par)
        tail(SND, tail_sum)
        tail(NEW, drain_result)
        tail(GAT, tail_pass)
        for w in range(WEIGHTS):
            half = whole[w].at[0]
            pltpu.make_async_copy(half, half, pal_recv.at[w]).wait()

    for z in range(CHIPS):

        @pl.when(chip == z)
        def _(z=z):
            body(z)


def communicate(terms, weights, m, v):
    def ring(dtype, *lead, of=WEIGHTS):
        return [pltpu.VMEM((*lead, *SHAPES[w]), dtype) for w in range(of)]

    def moments(arrays):
        return [(pltpu.VMEM if w == KEPT else jax.ShapeDtypeStruct)(a.shape, a.dtype) for w, a in enumerate(arrays)]

    dma = pltpu.SemaphoreType.DMA
    bf16, f32 = jnp.bfloat16, jnp.float32
    spaces = [pltpu.VMEM if w == KEPT else pl.ANY for w in range(WEIGHTS)]
    return pl.pallas_call(
        kernel,
        out_shape=[pltpu.VMEM(a.shape, a.dtype) for a in weights] + moments(m) + moments(v),
        in_specs=[pl.BlockSpec(memory_space=pl.ANY)] * (4 * WEIGHTS),
        out_specs=[pl.BlockSpec(memory_space=space) for space in (*[pltpu.VMEM] * WEIGHTS, *spaces, *spaces)],
        scratch_shapes=[
            *ring(bf16, CHIPS, OWN),
            *ring(bf16, CHIPS, PAR),
            *ring(bf16, CHIPS + 1, ARR),
            *ring(bf16, CHIPS, SND),
            *ring(f32, MOM),
            *ring(f32, MOM),
            *ring(bf16, MOM),
            *ring(f32, NEW, of=KEPT),
            *ring(f32, NEW, of=KEPT),
            dma((CHIPS, WEIGHTS, OWN)),
            dma((CHIPS, WEIGHTS, PAR)),
            dma((CHIPS, WEIGHTS, PAR)),
            dma((CHIPS + 1, WEIGHTS, ARR)),
            dma((CHIPS, WEIGHTS, SND)),
            dma((WEIGHTS, MOM)),
            dma((WEIGHTS, MOM)),
            dma((WEIGHTS, MOM)),
            dma((WEIGHTS, NEW)),
            dma((WEIGHTS, NEW)),
            dma((3, WEIGHTS, NEW)),
            dma((CHIPS, WEIGHTS, GAT)),
            dma((CHIPS, WEIGHTS, GAT)),
            dma((CHIPS, WEIGHTS, GAT)),
            dma((WEIGHTS,)),
        ],
        compiler_params=pltpu.CompilerParams(collective_id=0, has_side_effects=True, vmem_limit_bytes=GRANT),
        name="sum_step_gather",
    )(*terms, *weights, *m, *v)


def hand_out(arrays):
    kept = (0, 1, 2, 3 + KEPT, 6 + KEPT)
    rest = [n for n in range(9) if n not in kept]
    slots = 5

    def copy(*refs):
        given, out, buffer, into, out_of, sent = refs[:9], refs[9:18], *refs[18:]
        down = [pltpu.make_async_copy(given[n].at[l], out[n].at[l], sent.at[n, l]) for n in kept for l in range(2)]
        parts = [(n, l, pl.ds(half * 32, 32)) for n in rest for l in range(2) for half in range(2)]
        loads, stores = [], []
        for j, (n, l, rows) in enumerate(parts):
            slot = j % slots
            loads.append(pltpu.make_async_copy(given[n].at[l, rows], buffer.at[slot], into.at[slot]))
            stores.append(pltpu.make_async_copy(buffer.at[slot], out[n].at[l, rows], out_of.at[slot]))
        for load in loads[:slots]:
            load.start()
        for done in down:
            done.start()
        for j in range(len(parts)):
            loads[j].wait()
            stores[j].start()
            if j >= 2 and j - 2 + slots < len(parts):
                stores[j - 2].wait()
                loads[j - 2 + slots].start()
        for store in stores[-slots:]:
            store.wait()
        for done in down:
            done.wait()

    dma = pltpu.SemaphoreType.DMA
    return pl.pallas_call(
        copy,
        out_shape=[jax.ShapeDtypeStruct(a.shape, a.dtype) for a in arrays],
        in_specs=[pl.BlockSpec(memory_space=pl.ANY)] * 9,
        out_specs=[pl.BlockSpec(memory_space=pl.ANY)] * 9,
        scratch_shapes=[pltpu.VMEM((slots, 32, 8192), jnp.float32), dma((slots,)), dma((slots,)), dma((9, 2))],
        compiler_params=pltpu.CompilerParams(vmem_limit_bytes=GRANT),
        name="hand_out",
    )(*[pltpu.with_memory_space_constraint(a, pltpu.VMEM if n in kept else pltpu.HBM) for n, a in enumerate(arrays)])


def solution(mesh):
    def step(*arrays):
        terms, weights, m, v = (arrays[i : i + 3] for i in (0, 3, 6, 9))
        terms = [t.reshape(t.shape[1:]) for t in terms]
        return tuple(hand_out(communicate(terms, weights, m, v)))

    all_of, cut = P(None, None, None), P(None, "dp", None)
    return jax.shard_map(
        step,
        mesh=mesh,
        in_specs=(P(("rep", "dp"), None, None, None),) * 3 + (all_of,) * 3 + (cut,) * 6,
        out_specs=(P("rep", None, None),) * 3 + (P("rep", "dp", None),) * 6,
        check_vma=False,
    )
```

time: 617 us -> 591 us (0.958)
  Pallas kernels: 617 us -> 590 us
    pallas_call x2, Pallas kernels: 617 us -> 590 us  [the longest x1 560 us: communicate(): pl.pallas_call(kernel, out_shape=[pltpu.VMEM(a.shape, a.dtype) for a in w...]
where the time goes in v3:
time: 591 us
  Pallas kernels  590 us (100%)
    pallas_call x1, Pallas kernels, communicate(): pl.pallas_call(kernel, out_shape=[pltpu.VMEM(a.shape, a.dtype) for a in w...  560 us
    pallas_call x1, Pallas kernels, hand_out(): pl.pallas_call(copy, out_shape=[jax.ShapeDtypeStruct(a.shape, a.dtype) fo...  30.5 us

profile of v3, /device:TPU:0, one launch (start us, length us, event | category | flops | bytes accessed | tf_op | source)
XLA Modules:
  0.0 590.8 jit_solution(2439176804264800834)
XLA Ops:
  0.6 559.7 %sum_step_gather.1 = (bf16[2,512,8192]{2,1,0:T(8,128)(2,1)S(1)}, bf16[2,512,8192]{2,1,0:T(8,128)(2,1)S(1)}, bf16[2,8192,512]{2,1,0:T(8,128)(2,1)S(1)}, f32[2,64,...) custom-call(bf16[2,512,8192]{2,1,0:T(8,128)(2,1)} %bitcast.3, ...), custom_call_target="tpu_custom_call" | custom-call | tf_op jit(solution)/shard_map/sum_step_gather/pallas_call | solution.py:307
  560.3 30.5 %hand_out.1 = (bf16[2,512,8192]{2,1,0:T(8,128)(2,1)}, bf16[2,512,8192]{2,1,0:T(8,128)(2,1)}, bf16[2,8192,512]{2,1,0:T(8,128)(2,1)}, f32[2,64,8192]{2,1,0:T(8,128...) custom-call(bf16[2,512,8192]{2,1,0:T(8,128)(2,1)S(1)} %get-tuple-ele, ...), custom_call_target="tpu_custom_call" | custom-call | tf_op jit(solution)/shard_map/hand_out/pallas_call | solution.py:373

commit v4 on v3

--- a/solution.py
+++ b/solution.py
@@ -347,7 +347,12 @@
 
     def copy(*refs):
         given, out, buffer, into, out_of, sent = refs[:9], refs[9:18], *refs[18:]
-        down = [pltpu.make_async_copy(given[n].at[l], out[n].at[l], sent.at[n, l]) for n in kept for l in range(2)]
+        down = []
+        for part in range(8):
+            for n in kept:
+                rows = out[n].shape[1] // 4
+                where = part // 4, pl.ds(part % 4 * rows, rows)
+                down.append(pltpu.make_async_copy(given[n].at[where], out[n].at[where], sent.at[n, part]))
         parts = [(n, l, pl.ds(half * 32, 32)) for n in rest for l in range(2) for half in range(2)]
         loads, stores = [], []
         for j, (n, l, rows) in enumerate(parts):
@@ -356,11 +361,13 @@
             stores.append(pltpu.make_async_copy(buffer.at[slot], out[n].at[l, rows], out_of.at[slot]))
         for load in loads[:slots]:
             load.start()
-        for done in down:
+        for done in down[:8]:
             done.start()
         for j in range(len(parts)):
             loads[j].wait()
             stores[j].start()
+            for done in down[8 + 2 * j : 10 + 2 * j]:
+                done.start()
             if j >= 2 and j - 2 + slots < len(parts):
                 stores[j - 2].wait()
                 loads[j - 2 + slots].start()
@@ -375,7 +382,7 @@
         out_shape=[jax.ShapeDtypeStruct(a.shape, a.dtype) for a in arrays],
         in_specs=[pl.BlockSpec(memory_space=pl.ANY)] * 9,
         out_specs=[pl.BlockSpec(memory_space=pl.ANY)] * 9,
-        scratch_shapes=[pltpu.VMEM((slots, 32, 8192), jnp.float32), dma((slots,)), dma((slots,)), dma((9, 2))],
+        scratch_shapes=[pltpu.VMEM((slots, 32, 8192), jnp.float32), dma((slots,)), dma((slots,)), dma((9, 8))],
         compiler_params=pltpu.CompilerParams(vmem_limit_bytes=GRANT),
         name="hand_out",
     )(*[pltpu.with_memory_space_constraint(a, pltpu.VMEM if n in kept else pltpu.HBM) for n, a in enumerate(arrays)])

time: 591 us -> 590 us (level)
  no operation moved by 1% of the time
where the time goes in v4:
time: 590 us
  Pallas kernels  589 us (100%)
    pallas_call x1, Pallas kernels, communicate(): pl.pallas_call(kernel, out_shape=[pltpu.VMEM(a.shape, a.dtype) for a in w...  560 us
    pallas_call x1, Pallas kernels, hand_out(): pl.pallas_call(copy, out_shape=[jax.ShapeDtypeStruct(a.shape, a.dtype) fo...  29.7 us

profile of v4, /device:TPU:0, one launch (start us, length us, event | category | flops | bytes accessed | tf_op | source)
XLA Modules:
  0.0 590.1 jit_solution(3849882622693310393)
XLA Ops:
  0.6 559.7 %sum_step_gather.1 = (bf16[2,512,8192]{2,1,0:T(8,128)(2,1)S(1)}, bf16[2,512,8192]{2,1,0:T(8,128)(2,1)S(1)}, bf16[2,8192,512]{2,1,0:T(8,128)(2,1)S(1)}, f32[2,64,...) custom-call(bf16[2,512,8192]{2,1,0:T(8,128)(2,1)} %bitcast.3, ...), custom_call_target="tpu_custom_call" | custom-call | tf_op jit(solution)/shard_map/sum_step_gather/pallas_call | solution.py:307
  560.3 29.7 %hand_out.1 = (bf16[2,512,8192]{2,1,0:T(8,128)(2,1)}, bf16[2,512,8192]{2,1,0:T(8,128)(2,1)}, bf16[2,8192,512]{2,1,0:T(8,128)(2,1)}, f32[2,64,8192]{2,1,0:T(8,128...) custom-call(bf16[2,512,8192]{2,1,0:T(8,128)(2,1)S(1)} %get-tuple-ele, ...), custom_call_target="tpu_custom_call" | custom-call | tf_op jit(solution)/shard_map/hand_out/pallas_call | solution.py:380

commit v5 on v4

--- a/solution.py
+++ b/solution.py
@@ -10,7 +10,7 @@
 MESH = pl.DeviceIdType.MESH
 CHIPS = 4
 LAG = 2
-LEAD = 2
+LEAD = 4
 AHEAD = 3
 OWN, PAR, ARR, SND, MOM, NEW, GAT = 2, 3, 3, 2, 2, 2, 4
 WEIGHTS = 3

time: 590 us -> 590 us (level)
  no operation moved by 1% of the time
where the time goes in v5:
time: 590 us
  Pallas kernels  589 us (100%)
    pallas_call x1, Pallas kernels, communicate(): pl.pallas_call(kernel, out_shape=[pltpu.VMEM(a.shape, a.dtype) for a in w...  560 us
    pallas_call x1, Pallas kernels, hand_out(): pl.pallas_call(copy, out_shape=[jax.ShapeDtypeStruct(a.shape, a.dtype) fo...  29.7 us

profile of v5, /device:TPU:0, one launch (start us, length us, event | category | flops | bytes accessed | tf_op | source)
XLA Modules:
  0.0 590.0 jit_solution(4948271570847421231)
XLA Ops:
  0.6 559.6 %sum_step_gather.1 = (bf16[2,512,8192]{2,1,0:T(8,128)(2,1)S(1)}, bf16[2,512,8192]{2,1,0:T(8,128)(2,1)S(1)}, bf16[2,8192,512]{2,1,0:T(8,128)(2,1)S(1)}, f32[2,64,...) custom-call(bf16[2,512,8192]{2,1,0:T(8,128)(2,1)} %bitcast.3, ...), custom_call_target="tpu_custom_call" | custom-call | tf_op jit(solution)/shard_map/sum_step_gather/pallas_call | solution.py:307
  560.2 29.7 %hand_out.1 = (bf16[2,512,8192]{2,1,0:T(8,128)(2,1)}, bf16[2,512,8192]{2,1,0:T(8,128)(2,1)}, bf16[2,8192,512]{2,1,0:T(8,128)(2,1)}, f32[2,64,8192]{2,1,0:T(8,128...) custom-call(bf16[2,512,8192]{2,1,0:T(8,128)(2,1)S(1)} %get-tuple-ele, ...), custom_call_target="tpu_custom_call" | custom-call | tf_op jit(solution)/shard_map/hand_out/pallas_call | solution.py:380
